TPU v7x, 64 devices: a 2x2x8 block of a 4x4x8 slice. The times are simulated.
64 devices in a mesh: rep: 8 (over x, y, core), dp: 8 (over z).
Axes of the slice: x: 2, y: 2, z: 8, core: 2. Of those that a mesh axis runs over, the one named last changes fastest.
The devices are a block of a 4x4x8 slice.
Arguments:
- x: bfloat16 [64, 4096, 512], P(('rep', 'dp')), parts along dimension 0
- dy: bfloat16 [64, 4096, 512], P(('rep', 'dp')), parts along dimension 0
- w_gate: bfloat16 [2, 512, 1664], replicated
- w_up: bfloat16 [2, 512, 1664], replicated
- w_down: bfloat16 [2, 1664, 512], replicated
- m_w_gate: float32 [2, 512, 1664], replicated
- m_w_up: float32 [2, 512, 1664], replicated
- m_w_down: float32 [2, 1664, 512], replicated
- v_w_gate: float32 [2, 512, 1664], replicated
- v_w_up: float32 [2, 512, 1664], replicated
- v_w_down: float32 [2, 1664, 512], replicated
Outputs:
- output 1: bfloat16 [16, 512, 1664], P('rep'), parts along dimension 0
- output 2: bfloat16 [16, 512, 1664], P('rep'), parts along dimension 0
- output 3: bfloat16 [16, 1664, 512], P('rep'), parts along dimension 0
- output 4: float32 [16, 512, 1664], P('rep'), parts along dimension 0
- output 5: float32 [16, 512, 1664], P('rep'), parts along dimension 0
- output 6: float32 [16, 1664, 512], P('rep'), parts along dimension 0
- output 7: float32 [16, 512, 1664], P('rep'), parts along dimension 0
- output 8: float32 [16, 512, 1664], P('rep'), parts along dimension 0
- output 9: float32 [16, 1664, 512], P('rep'), parts along dimension 0
There are 8 independent parts. A program takes and returns all parts, laid end to end along the dimension named above; an argument that names none is the same for every part.
All inputs are finite; a program needn't handle non-finite values.
Results may differ from a plain program's by a relative error of at most 0.022.
Values are sent between devices in bfloat16 or wider.
A program may use at most 768 MiB of HBM per device.

v0:
```python
import jax
import jax.numpy as jnp
from jax import lax
from jax.sharding import PartitionSpec as P

NAMES = ("w_gate", "w_up", "w_down")


def matmul(a, w):
    return jnp.dot(a, w, preferred_element_type=jnp.float32).astype(jnp.bfloat16)


def normed(h):
    wide = h.astype(jnp.float32)
    scale = lax.rsqrt(jnp.mean(wide**2, -1, keepdims=True) + 1e-6)
    return (wide * scale).astype(jnp.bfloat16)


def layer(h, w):
    a = normed(h)
    gate = jnp.dot(a, w["w_gate"], preferred_element_type=jnp.float32)
    up = jnp.dot(a, w["w_up"], preferred_element_type=jnp.float32)
    return h + matmul((jax.nn.silu(gate) * up).astype(jnp.bfloat16), w["w_down"])


def adamw(w, m, v, g):
    m = 0.9 * m + 0.1 * g
    v = 0.95 * v + 0.05 * g * g
    step = m * lax.rsqrt(v + 1e-8) + 0.1 * w
    return (w - 0.02 * step).astype(jnp.bfloat16), m, v


def clipped(gradients, sum_of_squares, count):
    factor = jnp.minimum(1.0, 0.5 * lax.rsqrt(sum_of_squares / count + 1e-30))
    return [g * factor for g in gradients]


def solution(mesh):
    def step(x, dy, *arrays):
        weights, m, v = (arrays[i : i + 3] for i in (0, 3, 6))
        layers = weights[0].shape[0]
        h, kept = x[0], []
        for number in range(layers):
            kept.append(h)
            h = layer(h, {name: w[number] for name, w in zip(NAMES, weights, strict=True)})
        by_h, summed = dy[0], [None] * layers
        for number in reversed(range(layers)):
            _, back = jax.vjp(lambda w, h: layer(h, w), {name: w[number] for name, w in zip(NAMES, weights, strict=True)}, kept[number])
            by_w, by_h = back(by_h)
            summed[number] = [lax.psum(by_w[name], "dp") for name in NAMES]
        gradients = [jnp.stack([summed[number][i] for number in range(layers)]).astype(jnp.float32) for i in range(3)]
        gradients = clipped(gradients, sum(jnp.sum(g * g) for g in gradients), sum(g.size for g in gradients))
        new = [adamw(w.astype(jnp.float32), m, v, g) for w, m, v, g in zip(weights, m, v, gradients, strict=True)]
        return tuple(one[which] for which in range(3) for one in new)

    return jax.shard_map(
        step,
        mesh=mesh,
        in_specs=(P(("rep", "dp"), None, None),) * 2 + (P(None, None, None),) * 9,
        out_specs=(P("rep", None, None),) * 9,
        check_vma=False,
    )
```

profile of v0, /device:TPU:30, one launch (start us, length us, event | category | flops | bytes accessed | tf_op | source)
XLA Modules:
  0.0 574.4 jit_solution(6195412975347842450)
XLA Ops:
  7.2 0.1 all-reduce.3.cloned.1.call-start
  7.3 6.3 %copy.20 = bf16[1,4096,512]{1,2,0:T(8,128)(2,1)} copy(bf16[1,4096,512]{2,1,0:T(8,128)(2,1)} %param.11) | data formatting | bytes 8388608 | tf_op args[0]
  13.6 3.2 fusion.15
  16.8 0.0 copy-start.19
  16.8 6.3 %copy.21 = bf16[1,4096,512]{1,2,0:T(8,128)(2,1)} copy(bf16[1,4096,512]{2,1,0:T(8,128)(2,1)} %param.12) | data formatting | bytes 8388608 | tf_op args[1]
  23.2 12.5 %convolution_convert_fusion.1 = bf16[4096,1664]{1,0:T(8,128)(2,1)} fusion(bf16[1,4096,512]{2,1,0:T(8,128)(2,1)} %param.12, bf16[2,1664,512]{2,1,0:T(8,128)(2,1)S(1)} %copy-done.9), kind=kOutput, calls=%fused_computation.23 | convolution fusion | flops 6986137600 | bytes 19529728 | tf_op jit(solution)/shard_map/transpose(jvp())/dot_general | solution.py:10
  35.7 13.0 %fusion.94 = f32[4096,1664]{1,0:T(8,128)} fusion(bf16[2,512,1664]{2,1,0:T(8,128)(2,1)S(1)} %copy-done.11, bf16[1,4096,512]{2,1,0:T(8,128)(2,1)S(1)} %copy-done.5, f32[4096]{0:T(1024)S(1)} %add_rsqrt_fusion), kind=kOutput, calls=%fused_computation.112 | convolution fusion | flops 6985613312 | bytes 33177600 | tf_op jit(solution)/shard_map/dot_general | solution.py:21
  48.7 27.4 %multiply_convert_fusion.1 = (bf16[4096,1664]{1,0:T(8,128)(2,1)}, f32[4096,1664]{1,0:T(8,128)}) fusion(f32[4096,1664]{1,0:T(8,128)} %fusion.94, bf16[2,512,1664]{2,1,0:T(8,128)(2,1)} %param.14, bf16[1,4096,512]{2,1,0:T(8,128)(2,1)} %param.11, f32[4096]{0:T(1024)S(1)} %add_rsqrt_fusion), kind=kOutput, calls=%fused_computation.17 | convolution fusion | flops 7026507776 | bytes 74072064 | tf_op jit(solution)/shard_map/dot_general | solution.py:22
  76.1 12.5 %fusion.19 = (f32[4096]{0:T(1024)S(1)}, bf16[4096,512]{0,1:T(8,128)(2,1)S(1)}) fusion(bf16[4096,1664]{1,0:T(8,128)(2,1)} %get-tuple-element.24, bf16[2,1664,512]{2,1,0:T(8,128)(2,1)S(1)} %copy-done.9, bf16[1,4096,512]{1,2,0:T(8,128)(2,1)} %copy.20), kind=kOutput, calls=%fused_computation.52 | convolution fusion | flops 6989803520 | bytes 23740416 | tf_op jit(solution)/shard_map/dot_general | solution.py:10
  88.7 0.0 copy-start.7
  88.7 0.0 copy-start.17
  88.7 2.0 copy-done.7
  90.7 13.0 %fusion.81 = f32[4096,1664]{1,0:T(8,128)} fusion(bf16[4096,512]{0,1:T(8,128)(2,1)S(1)} %get-tuple-element.27, f32[4096]{0:T(1024)S(1)} %fusion.107, bf16[2,512,1664]{2,1,0:T(8,128)(2,1)S(1)} %copy-done.14), kind=kOutput, calls=%fused_computation.101 | convolution fusion | flops 6985613312 | bytes 33177600 | tf_op jit(solution)/shard_map/jvp()/dot_general | solution.py:22
  103.7 34.2 %fusion.2 = (bf16[4096,1664]{1,0:T(8,128)(2,1)}, f32[4096,1664]{1,0:T(8,128)}) fusion(f32[4096,1664]{1,0:T(8,128)} %fusion.81, bf16[4096,1664]{1,0:T(8,128)(2,1)} %convolution_convert_fusion.1, bf16[2,512,1664]{2,1,0:T(8,128)(2,1)} %param.13, bf16[4096,512]{0,1:T(8,128)(2,1)} %copy-done.7, f32[4096]{0:T(1024)S(1)} %fusion.107), kind=kOutput, calls=%fused_computation.8 | convolution fusion | flops 7067402240 | bytes 87703552 | tf_op jit(solution)/shard_map/jvp()/dot_general | solution.py:21
  137.9 20.5 %fusion.65 = bf16[1,1664,512]{2,1,0:T(8,128)(2,1)} fusion(bf16[1,4096,512]{2,1,0:T(8,128)(2,1)S(1)} %copy-done.6, f32[4096,1664]{1,0:T(8,128)} %fusion.81, f32[4096,1664]{1,0:T(8,128)} %get-tuple-element.29), kind=kOutput, calls=%fused_computation.95 | convolution fusion | flops 7021068288 | bytes 60424192 | tf_op jit(solution)/shard_map/transpose(jvp())/dot_general | solution.py:10
  158.4 19.9 %fusion.69 = bf16[1,512,1664]{2,1,0:T(8,128)(2,1)} fusion(bf16[4096,1664]{1,0:T(8,128)(2,1)} %convolution_convert_fusion.1, bf16[4096,512]{0,1:T(8,128)(2,1)} %copy-done.7, f32[4096]{0:T(1024)S(1)} %fusion.107, f32[4096,1664]{1,0:T(8,128)} %get-tuple-element.29), kind=kOutput, calls=%fused_computation.97 | convolution fusion | flops 7027359744 | bytes 46809088 | tf_op jit(solution)/shard_map/transpose(jvp())/dot_general | solution.py:22
  178.3 19.3 %fusion.43 = bf16[4096,512]{0,1:T(8,128)(2,1)} fusion(bf16[4096,1664]{1,0:T(8,128)(2,1)} %convolution_convert_fusion.1, bf16[2,512,1664]{2,1,0:T(8,128)(2,1)S(1)} %copy-done.15, f32[4096,1664]{1,0:T(8,128)} %get-tuple-element.29), kind=kOutput, calls=%fused_computation.77 | convolution fusion | flops 7022313472 | bytes 46792704 | tf_op jit(solution)/shard_map/transpose(jvp())/dot_general | solution.py:22
  197.6 14.5 %fusion.75 = bf16[1,512,1664]{2,1,0:T(8,128)(2,1)} fusion(bf16[4096,1664]{1,0:T(8,128)(2,1)} %get-tuple-element.28, bf16[4096,512]{0,1:T(8,128)(2,1)} %copy-done.7, f32[4096]{0:T(1024)S(1)} %fusion.107), kind=kOutput, calls=%fused_computation.99 | convolution fusion | flops 6985613312 | bytes 19546112 | tf_op jit(solution)/shard_map/transpose(jvp())/dot_general | solution.py:21
  212.1 12.1 %fusion.21 = (f32[4096]{0:T(1024)S(1)}, bf16[4096,512]{0,1:T(8,128)(2,1)S(1)}) fusion(bf16[4096,512]{0,1:T(8,128)(2,1)S(1)} %copy-done.8, bf16[4096,512]{0,1:T(8,128)(2,1)} %fusion.43, bf16[4096,1664]{1,0:T(8,128)(2,1)} %get-tuple-element.28, bf16[2,512,1664]{2,1,0:T(8,128)(2,1)S(1)} %copy-done.12), kind=kOutput, calls=%fused_computation.54 | convolution fusion | flops 6989803520 | bytes 27934720 | tf_op jit(solution)/shard_map/transpose(jvp())/dot_general | solution.py:21
  224.3 3.1 fusion.48
  227.4 12.3 %fusion.68 = bf16[1,1664,512]{2,1,0:T(8,128)(2,1)} fusion(bf16[4096,1664]{1,0:T(8,128)(2,1)} %get-tuple-element.24, bf16[4096,512]{0,1:T(8,128)(2,1)S(1)} %fusion.48), kind=kOutput, calls=%fused_computation.96 | convolution fusion | flops 6980173824 | bytes 19529728 | tf_op jit(solution)/shard_map/transpose(jvp())/dot_general | solution.py:10
  239.7 10.9 %convolution_convert_fusion = bf16[4096,1664]{1,0:T(8,128)(2,1)} fusion(bf16[4096,512]{0,1:T(8,128)(2,1)S(1)} %fusion.48, bf16[2,1664,512]{2,1,0:T(8,128)(2,1)S(1)} %copy-done.10), kind=kOutput, calls=%fused_computation.22 | convolution fusion | flops 6986137600 | bytes 19529728 | tf_op jit(solution)/shard_map/transpose(jvp())/dot_general | solution.py:10
  250.6 20.0 %fusion.76 = bf16[1,512,1664]{2,1,0:T(8,128)(2,1)} fusion(bf16[4096,1664]{1,0:T(8,128)(2,1)} %convolution_convert_fusion, f32[4096,1664]{1,0:T(8,128)} %fusion.94, bf16[1,4096,512]{1,2,0:T(8,128)(2,1)} %copy.20, f32[4096]{0:T(1024)S(1)} %copy-done.20), kind=kOutput, calls=%fused_computation.100 | convolution fusion | flops 7027359744 | bytes 46809088 | tf_op jit(solution)/shard_map/transpose(jvp())/dot_general | solution.py:22
  270.5 27.0 %fusion.70 = bf16[1,512,1664]{2,1,0:T(8,128)(2,1)} fusion(f32[4096,1664]{1,0:T(8,128)} %fusion.94, f32[4096,1664]{1,0:T(8,128)} %get-tuple-element.25, bf16[4096,1664]{1,0:T(8,128)(2,1)} %convolution_convert_fusion, bf16[1,4096,512]{1,2,0:T(8,128)(2,1)} %copy.20, f32[4096]{0:T(1024)S(1)} %copy-done.20), kind=kOutput, calls=%fused_computation.98 | convolution fusion | flops 7061438464 | bytes 74072064 | tf_op jit(solution)/shard_map/transpose(jvp())/dot_general | solution.py:21
  297.6 0.1 all-reduce.3.cloned.1.call-update
  297.7 219.5 %all-reduce.3.cloned.1.call-done = (bf16[1,512,1664]{2,1,0:T(8,128)(2,1)}, bf16[1,512,1664]{2,1,0:T(8,128)(2,1)}, bf16[1,512,1664]{2,1,0:T(8,128)(2,1)}, bf16[1,...) async-done(((bf16[1,512,1664]{2,1,0:T(8,128)(2,1)}, bf16[1,512,1664]{2,1,0:T(8,128)(2,1)}, bf16[1,512,1664]{2,1,0:T(8,128)(2,1)}, ...) | async-done | bytes 10223632 | tf_op jit(solution)/shard_map/psum | solution.py:50
  517.2 4.5 fusion.33
  521.7 4.3 fusion.32
  526.0 2.4 fusion.31
  530.4 14.4 %fusion.39 = (bf16[2,1664,512]{2,1,0:T(8,128)(2,1)}, f32[2,1664,512]{2,1,0:T(8,128)}, f32[2,1664,512]{2,1,0:T(8,128)}) fusion(bf16[2,1664,512]{2,1,0:T(8,128)(2,1)} %param.15, f32[]{:T(128)S(6)} %min_shard_map.3, bf16[1,1664,512]{2,1,0:T(8,128)(2,1)} %get-tuple-element.13, bf16[1,1664,512]{2,1,0:T(8,128)(2,1)} %get-tuple-element.14, ...), kind=kLoop, calls=%fused_computation.73 | loop fusion | flops 34078720 | bytes 37486596 | tf_op jit(solution)/shard_map/convert_element_type | solution.py:30
  544.8 1.2 copy-done.16
  546.0 21.1 %fusion.30 = (bf16[2,512,1664]{2,1,0:T(8,128)(2,1)}, f32[2,512,1664]{2,1,0:T(8,128)}, f32[2,512,1664]{2,1,0:T(8,128)}, bf16[2,512,1664]{2,1,0:T(8,128)(2,1)}, f3...) fusion(bf16[2,512,1664]{2,1,0:T(8,128)(2,1)S(1)} %copy-done.13, f32[]{:T(128)S(6)} %min_shard_map.3, ...), kind=kLoop, calls=%fused_computation.64 | loop fusion | flops 68157440 | bytes 74973184 | tf_op jit(solution)/shard_map/convert_element_type | solution.py:30
  (40 shorter events, 0.1 us)
Async XLA Ops:
  7.2 510.0 %all-reduce.3.cloned.1.call-start = ((), (), s32[]{:S(2)}) async-start(), calls=%async_computation | async-start | bytes 20447232 | tf_op jit(solution)/shard_map/psum | solution.py:50
  13.6 9.6 %copy-start.9 = (bf16[2,1664,512]{2,1,0:T(8,128)(2,1)S(1)}, bf16[2,1664,512]{2,1,0:T(8,128)(2,1)}, u32[]{:S(2)}) copy-start(bf16[2,1664,512]{2,1,0:T(8,128)(2,1)} %param.15) | copy-start | bytes 10223620
  16.8 31.9 %copy-start.19 = (f32[4096]{0:T(1024)}, f32[4096]{0:T(1024)S(1)}, u32[]{:S(2)}) copy-start(f32[4096]{0:T(1024)S(1)} %add_rsqrt_fusion) | copy-start | bytes 49156
  23.2 12.5 %copy-start.5 = (bf16[1,4096,512]{2,1,0:T(8,128)(2,1)S(1)}, bf16[1,4096,512]{2,1,0:T(8,128)(2,1)}, u32[]{:S(2)}) copy-start(bf16[1,4096,512]{2,1,0:T(8,128)(2,1)} %param.11) | copy-start | bytes 12582916
  23.2 12.5 %copy-start.11 = (bf16[2,512,1664]{2,1,0:T(8,128)(2,1)S(1)}, bf16[2,512,1664]{2,1,0:T(8,128)(2,1)}, u32[]{:S(2)}) copy-start(bf16[2,512,1664]{2,1,0:T(8,128)(2,1)} %param.13) | copy-start | bytes 10223620
  76.1 14.5 %copy-start.14 = (bf16[2,512,1664]{2,1,0:T(8,128)(2,1)S(1)}, bf16[2,512,1664]{2,1,0:T(8,128)(2,1)}, u32[]{:S(2)}) copy-start(bf16[2,512,1664]{2,1,0:T(8,128)(2,1)} %param.14) | copy-start | bytes 10223620
  88.7 2.0 copy-start.7
  88.7 2.0 copy-start.17
  103.7 34.2 %copy-start.6 = (bf16[1,4096,512]{2,1,0:T(8,128)(2,1)S(1)}, bf16[1,4096,512]{2,1,0:T(8,128)(2,1)}, u32[]{:S(2)}) copy-start(bf16[1,4096,512]{2,1,0:T(8,128)(2,1)} %param.12) | copy-start | bytes 12582916
  158.4 19.9 %copy-start.15 = (bf16[2,512,1664]{2,1,0:T(8,128)(2,1)S(1)}, bf16[2,512,1664]{2,1,0:T(8,128)(2,1)}, u32[]{:S(2)}) copy-start(bf16[2,512,1664]{2,1,0:T(8,128)(2,1)} %param.14) | copy-start | bytes 10223620
  197.6 14.5 %copy-start.8 = (bf16[4096,512]{0,1:T(8,128)(2,1)S(1)}, bf16[4096,512]{0,1:T(8,128)(2,1)}, u32[]{:S(2)}) copy-start(bf16[4096,512]{0,1:T(8,128)(2,1)} %copy-done.7) | copy-start | bytes 12582916
  197.6 14.5 %copy-start.12 = (bf16[2,512,1664]{2,1,0:T(8,128)(2,1)S(1)}, bf16[2,512,1664]{2,1,0:T(8,128)(2,1)}, u32[]{:S(2)}) copy-start(bf16[2,512,1664]{2,1,0:T(8,128)(2,1)} %param.13) | copy-start | bytes 10223620
  212.1 12.2 %copy-start.18 = (f32[4096]{0:T(1024)S(1)}, f32[4096]{0:T(1024)}, u32[]{:S(2)}) copy-start(f32[4096]{0:T(1024)} %copy-done.17) | copy-start | bytes 49156
  212.1 12.2 %copy-start = (bf16[1,4096,512]{1,2,0:T(8,128)(2,1)S(1)}, bf16[1,4096,512]{1,2,0:T(8,128)(2,1)}, u32[]{:S(2)}) copy-start(bf16[1,4096,512]{1,2,0:T(8,128)(2,1)} %copy.21) | copy-start | bytes 12582916
  227.4 12.3 %copy-start.10 = (bf16[2,1664,512]{2,1,0:T(8,128)(2,1)S(1)}, bf16[2,1664,512]{2,1,0:T(8,128)(2,1)}, u32[]{:S(2)}) copy-start(bf16[2,1664,512]{2,1,0:T(8,128)(2,1)} %param.15) | copy-start | bytes 10223620
  239.7 10.9 %copy-start.20 = (f32[4096]{0:T(1024)S(1)}, f32[4096]{0:T(1024)}, u32[]{:S(2)}) copy-start(f32[4096]{0:T(1024)} %copy-done.19) | copy-start | bytes 49156
  517.2 8.8 %copy-start.1 = (bf16[1,512,1664]{2,1,0:T(8,128)(2,1)S(1)}, bf16[1,512,1664]{2,1,0:T(8,128)(2,1)}, u32[]{:S(2)}) copy-start(bf16[1,512,1664]{2,1,0:T(8,128)(2,1)} %get-tuple-element.9) | copy-start | bytes 5111812
  517.2 8.8 %copy-start.2 = (bf16[1,512,1664]{2,1,0:T(8,128)(2,1)S(1)}, bf16[1,512,1664]{2,1,0:T(8,128)(2,1)}, u32[]{:S(2)}) copy-start(bf16[1,512,1664]{2,1,0:T(8,128)(2,1)} %get-tuple-element.10) | copy-start | bytes 5111812
  530.3 14.5 %copy-start.3 = (bf16[1,512,1664]{2,1,0:T(8,128)(2,1)S(1)}, bf16[1,512,1664]{2,1,0:T(8,128)(2,1)}, u32[]{:S(2)}) copy-start(bf16[1,512,1664]{2,1,0:T(8,128)(2,1)} %get-tuple-element.11) | copy-start | bytes 5111812
  530.3 14.5 %copy-start.4 = (bf16[1,512,1664]{2,1,0:T(8,128)(2,1)S(1)}, bf16[1,512,1664]{2,1,0:T(8,128)(2,1)}, u32[]{:S(2)}) copy-start(bf16[1,512,1664]{2,1,0:T(8,128)(2,1)} %get-tuple-element.12) | copy-start | bytes 5111812
  530.4 14.5 %copy-start.13 = (bf16[2,512,1664]{2,1,0:T(8,128)(2,1)S(1)}, bf16[2,512,1664]{2,1,0:T(8,128)(2,1)}, u32[]{:S(2)}) copy-start(bf16[2,512,1664]{2,1,0:T(8,128)(2,1)} %param.13) | copy-start | bytes 10223620
  530.4 15.7 %copy-start.16 = (bf16[2,512,1664]{2,1,0:T(8,128)(2,1)S(1)}, bf16[2,512,1664]{2,1,0:T(8,128)(2,1)}, u32[]{:S(2)}) copy-start(bf16[2,512,1664]{2,1,0:T(8,128)(2,1)} %param.14) | copy-start | bytes 10223620
Sparse Core Ops, SparseCore 0:
  297.8 219.3 all-reduce.2
where the time goes:
time: 583 us; the launch traced here: 574 us
  matrix products  269 us (46%)
  waiting for transfers between devices  220 us (38%)
  other arithmetic  53 us (9%)
  between operations  16.7 us (3%)
  local copies, waits for them, and re-layouts  15.9 us (3%)
    psum x1, waiting for transfers between devices, step(): summed[number] = [lax.psum(by_w[name], 'dp') for name in NAMES]  220 us
    dot_general x5, matrix products, layer(): gate = jnp.dot(a, w['w_gate'], preferred_element_type=jnp.float32)  101 us
    dot_general x5, matrix products, layer(): up = jnp.dot(a, w['w_up'], preferred_element_type=jnp.float32)  99.5 us
    dot_general x5, matrix products, matmul(): jnp.dot(a, w, preferred_element_type=jnp.float32).astype(jnp.bfloat16)  68.7 us
    convert_element_type x2, other arithmetic, adamw(): return ((w - 0.02 * step).astype(jnp.bfloat16), m, v)  35.5 us
    unnamed x44, local copies, waits for them, and re-layouts  15.9 us
  transfers between devices with their start and end apart: 1, of which 1 were waited for; matrix products, arithmetic and copies ran while one was open for 0% of the time, Pallas kernels for 0%

commit v1 on v0

v1 whole, which is shorter than its diff:
```python
import functools

import jax
import jax.numpy as jnp
from jax import lax
from jax.experimental import pallas as pl
from jax.experimental.pallas import tpu as pltpu
from jax.sharding import PartitionSpec as P

MESH = pl.DeviceIdType.MESH
LANES = 128
KINDS = 3
WIDE = 2
SLOTS = 4
F32, BF16 = jnp.float32, jnp.bfloat16


def nn(a, b):
    return lax.dot_general(a, b, (((1,), (0,)), ((), ())), preferred_element_type=F32)


def nt(a, b):
    return lax.dot_general(a, b, (((1,), (1,)), ((), ())), preferred_element_type=F32)


def tn(a, b):
    return lax.dot_general(a, b, (((0,), (0,)), ((), ())), preferred_element_type=F32)


def sigmoid(x):
    return 0.5 * jnp.tanh(0.5 * x) + 0.5


def normed(h):
    wide = h.astype(F32)
    scale = lax.rsqrt(jnp.mean(wide * wide, -1, keepdims=True) + 1e-6)
    return (wide * scale).astype(BF16)


def normed_back(h, da):
    wide, da = h.astype(F32), da.astype(BF16).astype(F32)
    scale = lax.rsqrt(jnp.mean(wide * wide, -1, keepdims=True) + 1e-6)
    return (scale * (da - wide * (scale * scale * jnp.mean(da * wide, -1, keepdims=True)))).astype(BF16)


def gradients_kernel(
    n, x_hbm, dy_hbm, wg_hbm, wu_hbm, wd_hbm, g_hbm, squares_ref,
    a0, h1, a1, dh, wg, wu, wd, da, acc, part, recv, own_squares, all_squares,
    load_x, load_dy, load_w, send_sem, recv_sem, keep_sem, sq_send, sq_recv,
):
    tokens, d = x_hbm.shape
    ff = wg.shape[-1]
    blocks = ff // LANES
    per_layer = (blocks + 1) // WIDE
    pieces = 2 * per_layer
    rows = KINDS * LANES // n
    tiles = load_x.shape[0]
    tile = tokens // tiles
    me = lax.axis_index("dp")

    def load_tile(hbm, ref, sem, i):
        at = pl.ds(pl.multiple_of(i * tile, tile), tile)
        return pltpu.make_async_copy(hbm.at[at], ref.at[at], sem.at[i])

    def load_weight(i, layer):
        hbm, ref = ((wg_hbm, wg), (wu_hbm, wu), (wd_hbm, wd))[i]
        return pltpu.make_async_copy(hbm.at[layer], ref.at[layer], load_w.at[layer, i])

    load_tile(x_hbm, a0, load_x, 0).start()
    for i in range(KINDS):
        load_weight(i, 0).start()
    for i in range(1, tiles):
        load_tile(x_hbm, a0, load_x, i).start()
    for i in range(KINDS):
        load_weight(i, 1).start()
    for i in range(tiles):
        load_tile(dy_hbm, dh, load_dy, i).start()

    barrier = pltpu.get_barrier_semaphore()
    for away in range(1, n):
        pl.semaphore_signal(barrier, inc=1, device_id={"dp": lax.rem(me + away, n)}, device_id_type=MESH)
    pl.semaphore_wait(barrier, n - 1)

    own_squares[...] = jnp.zeros_like(own_squares)

    for i in range(KINDS):
        load_weight(i, 0).wait()
    bounds = [(f, min(f + 2 * LANES, ff)) for f in range(0, ff, 2 * LANES)]

    def forward(i, _):
        load_tile(x_hbm, a0, load_x, i).wait()
        at = pl.ds(pl.multiple_of(i * tile, tile), tile)
        h = a0[at]
        a = normed(h)
        total = None
        for lo, hi in bounds:
            gate, up = nn(a, wg[0, :, lo:hi]), nn(a, wu[0, :, lo:hi])
            y = nn((gate * sigmoid(gate) * up).astype(BF16), wd[0, lo:hi, :])
            total = y if total is None else total + y
        h = (h.astype(F32) + total.astype(BF16).astype(F32)).astype(BF16)
        a0[at] = a
        h1[at] = h
        a1[at] = normed(h)
        da[at] = jnp.zeros((tile, d), F32)
        return 0

    lax.fori_loop(0, tiles, forward, 0)
    for i in range(KINDS):
        load_weight(i, 1).wait()
    for i in range(tiles):
        load_tile(dy_hbm, dh, load_dy, i).wait()

    def chunk(c):
        return pl.ds(pl.multiple_of(lax.rem(c + 2 * n, n) * rows, rows), rows)

    def copy_of(p, way, age, kind):
        block, sign = WIDE * p + way, 1 - 2 * way
        if kind == "sum":
            source = part.at[block, chunk(me - sign * (age + 1))]
            target = recv.at[block, age]
        else:
            at = chunk(me - sign * (age - (n - 1)))
            source = part.at[block, at] if kind == "first" else g_hbm.at[block, at]
            target = g_hbm.at[block, at]
        return pltpu.make_async_remote_copy(
            src_ref=source,
            dst_ref=target,
            send_sem=send_sem.at[block],
            recv_sem=recv_sem.at[block, age],
            device_id={"dp": lax.rem(me + sign + n, n)},
            device_id_type=MESH,
        )

    def arrived(p, way, age, kind):
        copy = copy_of(p, way, age, kind)
        copy.wait_send()
        if kind == "sum":
            copy.wait_recv()
        else:
            block, sign = WIDE * p + way, 1 - 2 * way
            at = chunk(me - sign * (age - (n - 1) + 1))
            pltpu.make_async_remote_copy(
                src_ref=g_hbm.at[block, at],
                dst_ref=g_hbm.at[block, at],
                send_sem=send_sem.at[block],
                recv_sem=recv_sem.at[block, age],
                device_id={"dp": lax.rem(me + sign + n, n)},
                device_id_type=MESH,
            ).wait_recv()

    def add(p, way, age):
        block, sign = WIDE * p + way, 1 - 2 * way
        at = chunk(me - sign * (age + 1))
        total = (part[block, at].astype(F32) + recv[block, age - 1].astype(F32)).astype(BF16)
        part[block, at] = total
        return total

    def keep(p, way):
        block = WIDE * p + way
        return pltpu.make_async_copy(part.at[block, chunk(me)], g_hbm.at[block, chunk(me)], keep_sem.at[block])

    def finish(p, way):
        total = add(p, way, n - 1).astype(F32)
        copy_of(p, way, n - 1, "first").start()
        keep(p, way).start()
        total = total * total
        squares = own_squares[...]
        for r in range(0, rows, 8):
            for c in range(0, d, LANES):
                squares = squares + total[r : r + 8, c : c + LANES]
        own_squares[...] = squares

    def move(p, way, age):
        last = 2 * (n - 1)

        @pl.when(age == 0)
        def _():
            copy_of(p, way, age, "sum").start()

        @pl.when((age >= 1) & (age <= n - 1))
        def _():
            arrived(p, way, age - 1, "sum")

            @pl.when(age < n - 1)
            def _():
                add(p, way, age)
                copy_of(p, way, age, "sum").start()

            @pl.when(age == n - 1)
            def _():
                finish(p, way)

        @pl.when(age == n)
        def _():
            arrived(p, way, age - 1, "first")

        @pl.when((age > n) & (age <= last))
        def _():
            arrived(p, way, age - 1, "whole")

        @pl.when((age >= n) & (age < last))
        def _():
            copy_of(p, way, age, "whole").start()

        @pl.when(age == last)
        def _():
            keep(p, way).wait()

    in_flight = -(-(2 * (n - 1) + 1) // SLOTS)

    def slot(s):
        def one(k, _):
            q = in_flight - 1 - k
            p, age = s // SLOTS - 1 - q, s % SLOTS + SLOTS * q

            @pl.when((p >= 0) & (p < pieces))
            def _():
                @pl.when(p != pieces - 1)
                def _():
                    move(p, 0, age)

                @pl.when(p != per_layer - 1)
                def _():
                    move(p, 1, age)

            return 0

        lax.fori_loop(0, in_flight, one, 0)

    def compute(layer, p, lo, wide, last):
        units = wide * LANES
        at_units = pl.ds(lo, units)
        a_ref = (a0, a1)[layer]
        acc[...] = jnp.zeros_like(acc)

        def some(i, _):
            for k in range(tiles // SLOTS):
                at = pl.ds(pl.multiple_of((i * (tiles // SLOTS) + k) * tile, tile), tile)
                w_gate, w_up, w_down = wg[layer, :, at_units], wu[layer, :, at_units], wd[layer, at_units, :]
                a, back = a_ref[at], dh[at]
                gate, up = nn(a, w_gate), nn(a, w_up)
                by_act = nt(back, w_down).astype(BF16).astype(F32)
                s = sigmoid(gate)
                silu = gate * s
                act = (silu * up).astype(BF16)
                by_up = (by_act * silu).astype(BF16)
                by_gate = (by_act * up * (s + silu * (1.0 - s))).astype(BF16)
                acc[0:units] += tn(act, back)
                acc[units : 2 * units] += tn(by_gate, a)
                acc[2 * units : 3 * units] += tn(by_up, a)
                if layer == 1:
                    total = da[at] + nt(by_gate, w_gate) + nt(by_up, w_up)
                    if last:
                        dh[at] = (back.astype(F32) + normed_back(h1[at], total).astype(F32)).astype(BF16)
                    else:
                        da[at] = total
            slot(p * SLOTS + i)
            return 0

        lax.fori_loop(0, SLOTS, some, 0)
        for half in range(wide):
            way = half if wide == WIDE else 1 - layer
            for kind in range(KINDS):
                first = kind * units + half * LANES
                part[WIDE * p + way, kind * LANES : (kind + 1) * LANES] = acc[first : first + LANES].astype(BF16)

    def chunk_of(layer, j, _):
        base = (1 - layer) * per_layer
        compute(layer, base + j, pl.multiple_of(j * WIDE * LANES, WIDE * LANES), WIDE, False)
        return 0

    for layer in (1, 0):
        lax.fori_loop(0, per_layer - 1, functools.partial(chunk_of, layer), 0)
        compute(layer, (2 - layer) * per_layer - 1, (blocks - 1) * LANES, 1, True)

    def rest(s, _):
        slot(s)
        return 0

    done = SLOTS * (pieces + 1) + 2 * (n - 1) + 1
    summed = SLOTS * (pieces + 1) - SLOTS + n + SLOTS
    lax.fori_loop(SLOTS * pieces, summed, rest, 0)

    def squares_to(away):
        return pltpu.make_async_remote_copy(
            src_ref=own_squares,
            dst_ref=all_squares.at[me],
            send_sem=sq_send.at[away],
            recv_sem=sq_recv.at[away],
            device_id={"dp": lax.rem(me + away, n)},
            device_id_type=MESH,
        )

    def squares_from(away):
        return pltpu.make_async_remote_copy(
            src_ref=own_squares,
            dst_ref=all_squares.at[lax.rem(me - away + n, n)],
            send_sem=sq_send.at[away],
            recv_sem=sq_recv.at[away],
            device_id={"dp": lax.rem(me + away, n)},
            device_id_type=MESH,
        )

    for away in range(1, n):
        squares_to(away).start()
    all_squares[me] = own_squares[...]
    lax.fori_loop(summed, done, rest, 0)
    for away in range(1, n):
        squares_to(away).wait_send()
        squares_from(away).wait_recv()
    total = all_squares[0]
    for i in range(1, n):
        total = total + all_squares[i]
    squares_ref[...] = total


def gradients(n, tiles, x, dy, w_gate, w_up, w_down):
    (tokens, d), (layers, _, ff) = x.shape, w_gate.shape
    blocks = 2 * WIDE * ((ff // LANES + 1) // WIDE)
    rows = KINDS * LANES // n
    states = pltpu.VMEM((tokens, d), BF16)
    dma = pltpu.SemaphoreType.DMA
    any_space = pl.BlockSpec(memory_space=pl.ANY)
    return pl.pallas_call(
        functools.partial(gradients_kernel, n),
        out_shape=(
            jax.ShapeDtypeStruct((blocks, KINDS * LANES, d), BF16),
            jax.ShapeDtypeStruct((8, LANES), F32),
        ),
        in_specs=[any_space] * 5,
        out_specs=(any_space, pl.BlockSpec(memory_space=pltpu.VMEM)),
        scratch_shapes=[
            states, states, states, states,
            pltpu.VMEM(w_gate.shape, BF16), pltpu.VMEM(w_up.shape, BF16), pltpu.VMEM(w_down.shape, BF16),
            pltpu.VMEM((tokens, d), F32),
            pltpu.VMEM((KINDS * WIDE * LANES, d), F32),
            pltpu.VMEM((blocks, KINDS * LANES, d), BF16),
            pltpu.VMEM((blocks, n - 1, rows, d), BF16),
            pltpu.VMEM((8, LANES), F32),
            pltpu.VMEM((n, 8, LANES), F32),
            dma((tiles,)), dma((tiles,)), dma((layers, KINDS)),
            dma((blocks,)), dma((blocks, 2 * (n - 1))), dma((blocks,)),
            dma((n,)), dma((n,)),
        ],
        compiler_params=pltpu.CompilerParams(
            collective_id=0, has_side_effects=True, vmem_limit_bytes=67_043_328
        ),
        name="gradients",
    )(x, dy, w_gate, w_up, w_down)


def step_kernel(count, squares_ref, g1_ref, g0_ref, *refs):
    old, new = refs[:9], refs[9:]
    mean = jnp.sum(jnp.sum(squares_ref[...], 0, keepdims=True), 1, keepdims=True) / count
    factor = jnp.minimum(1.0, 0.5 * lax.rsqrt(mean + 1e-30))
    for i, kind in enumerate((1, 2, 0)):
        for layer, g_ref in ((0, g0_ref), (1, g1_ref)):
            g = g_ref[0, kind * LANES : (kind + 1) * LANES, :].astype(F32)
            if kind:
                g = g.T
            g = g * factor
            m = 0.9 * old[3 + i][layer] + 0.1 * g
            v = 0.95 * old[6 + i][layer] + 0.05 * g * g
            w = old[i][layer].astype(F32)
            new[i][layer] = (w - 0.02 * (m * lax.rsqrt(v + 1e-8) + 0.1 * w)).astype(BF16)
            new[3 + i][layer] = m
            new[6 + i][layer] = v


def take_step(summed, squares, weights, m, v):
    layers, d, ff = weights[0].shape
    blocks = ff // LANES
    count = float(sum(w.size for w in weights))
    by_columns = pl.BlockSpec((layers, d, LANES), lambda f: (0, 0, f))
    by_rows = pl.BlockSpec((layers, LANES, d), lambda f: (0, f, 0))
    arrays = [by_columns, by_columns, by_rows] * 3
    block = (1, KINDS * LANES, d)
    half = summed.shape[0] // 2
    return pl.pallas_call(
        functools.partial(step_kernel, count),
        grid=(blocks,),
        out_shape=[jax.ShapeDtypeStruct(a.shape, a.dtype) for a in (*weights, *m, *v)],
        in_specs=[
            pl.BlockSpec((8, LANES), lambda f: (0, 0)),
            pl.BlockSpec(block, lambda f: (f, 0, 0)),
            pl.BlockSpec(block, lambda f: (half + f + f // (blocks - 1), 0, 0)),
            *arrays,
        ],
        out_specs=arrays,
        compiler_params=pltpu.CompilerParams(dimension_semantics=("arbitrary",), vmem_limit_bytes=50_000_000),
        name="step",
    )(squares, summed, summed, *weights, *m, *v)


def solution(mesh, tiles=8):
    n = mesh.shape["dp"]

    def step(x, dy, *arrays):
        weights, m, v = (arrays[i : i + 3] for i in (0, 3, 6))
        summed, squares = gradients(n, tiles, x[0], dy[0], *weights)
        return tuple(take_step(summed, squares, weights, m, v))

    return jax.shard_map(
        step,
        mesh=mesh,
        in_specs=(P(("rep", "dp"), None, None),) * 2 + (P(None, None, None),) * 9,
        out_specs=(P("rep", None, None),) * 9,
        check_vma=False,
    )
```

time: 583 us -> 373 us (0.64); the launches traced: 574 us -> 373 us
  Pallas kernels: 0 us -> 370 us
  matrix products: 269 us -> 0 us
  waiting for transfers between devices: 220 us -> 0 us
  other arithmetic: 53 us -> 0 us
  between operations: 16.7 us -> 0.82 us
  local copies, waits for them, and re-layouts: 15.9 us -> 2.63 us
    pallas_call x0 -> x2, Pallas kernels: none -> 370 us  [the longest x1 328 us: gradients(): pl.pallas_call(functools.partial(gradients_kernel, n), out_shape=(jax.Sha...]
    dot_general x15 -> x0, matrix products: 269 us -> none  [the longest x5 101 us: layer(): gate = jnp.dot(a, w['w_gate'], preferred_element_type=jnp.float32)]
    psum x1 -> x0, waiting for transfers between devices: 220 us -> none  [step(): summed[number] = [lax.psum(by_w[name], 'dp') for name in NAMES]]
    convert_element_type x2 -> x0, other arithmetic: 35.5 us -> none  [adamw(): return ((w - 0.02 * step).astype(jnp.bfloat16), m, v)]
    reduce_sum x4 -> x0, other arithmetic: 14.4 us -> none  [the longest x3 11.1 us: step(): jnp.sum(g * g)]
    unnamed x44 -> x4, local copies, waits for them, and re-layouts: 15.9 us -> 2.63 us
  transfers between devices with their start and end apart: 1 -> 0, of which waited for: 1 -> 0; matrix products, arithmetic and copies ran while one was open for 0% -> 0% of each run, Pallas kernels for 0% -> 0%
where the time goes in v1:
time: 373 us
  Pallas kernels  370 us (99%)
    pallas_call x1, Pallas kernels, gradients(): pl.pallas_call(functools.partial(gradients_kernel, n), out_shape=(jax.Sha...  328 us
    pallas_call x1, Pallas kernels, take_step(): pl.pallas_call(functools.partial(step_kernel, count), grid=(blocks,), out...  42.2 us

profile of v1, /device:TPU:30, one launch (start us, length us, event | category | flops | bytes accessed | tf_op | source)
XLA Modules:
  0.0 373.3 jit_solution(13838976489393742940)
XLA Ops:
  0.6 327.6 %gradients.1 = (bf16[28,384,512]{2,1,0:T(8,128)(2,1)}, f32[8,128]{1,0:T(8,128)}) custom-call(bf16[4096,512]{1,0:T(8,128)(2,1)} %bitcast.2, bf16[4096,512]{1,0:T(8,128)(2,1)} %bitcast.3, bf16[2,512,1664]{2,1,0:T(8,128)(2,1)} %refs_0_.1, bf16[2,512,1664]{2,1,0:T(8,128)(2,1)} %refs_1_.1, bf16[2,1664,512]{2,1,0:T(8,128)(2,1)} %refs_2_.1), custom_call_target="tpu_custom_call" | custom-call | tf_op jit(solution)/shard_map/gradients/pallas_call | solution.py:324
  328.3 0.0 copy-start
  328.3 2.0 copy-done
  330.3 0.0 copy-start.1
  330.3 0.7 copy-done.1
  330.9 42.2 %step.1 = (bf16[2,512,1664]{2,1,0:T(8,128)(2,1)}, bf16[2,512,1664]{2,1,0:T(8,128)(2,1)}, bf16[2,1664,512]{2,1,0:T(8,128)(2,1)}, f32[2,512,1664]{2,1,0:T(8,128)},...) custom-call(f32[8,128]{1,0:T(8,128)S(1)} %copy-done.1, ...), custom_call_target="tpu_custom_call" | custom-call | tf_op jit(solution)/shard_map/step/pallas_call | solution.py:379
Async XLA Ops:
  328.3 2.0 copy-start
  330.3 0.7 copy-start.1

commit v2 on v1

--- a/solution.py
+++ b/solution.py
@@ -11,7 +11,8 @@
 LANES = 128
 KINDS = 3
 WIDE = 2
-SLOTS = 4
+SLOTS = (2, 2)
+PAIR = 2
 F32, BF16 = jnp.float32, jnp.bfloat16
 
 
@@ -79,7 +80,6 @@
     barrier = pltpu.get_barrier_semaphore()
     for away in range(1, n):
         pl.semaphore_signal(barrier, inc=1, device_id={"dp": lax.rem(me + away, n)}, device_id_type=MESH)
-    pl.semaphore_wait(barrier, n - 1)
 
     own_squares[...] = jnp.zeros_like(own_squares)
 
@@ -110,116 +110,116 @@
     for i in range(tiles):
         load_tile(dy_hbm, dh, load_dy, i).wait()
 
+    pl.semaphore_wait(barrier, n - 1)
+
+    long, short = n // 2, n - 1 - n // 2
+    flows = ((0, long), (1, short))
+    last_age = 2 * long
+
     def chunk(c):
         return pl.ds(pl.multiple_of(lax.rem(c + 2 * n, n) * rows, rows), rows)
 
-    def copy_of(p, way, age, kind):
-        block, sign = WIDE * p + way, 1 - 2 * way
-        if kind == "sum":
-            source = part.at[block, chunk(me - sign * (age + 1))]
-            target = recv.at[block, age]
-        else:
-            at = chunk(me - sign * (age - (n - 1)))
-            source = part.at[block, at] if kind == "first" else g_hbm.at[block, at]
-            target = g_hbm.at[block, at]
+    def copy_of(block, sign, flow, age, source, target):
         return pltpu.make_async_remote_copy(
             src_ref=source,
             dst_ref=target,
-            send_sem=send_sem.at[block],
-            recv_sem=recv_sem.at[block, age],
+            send_sem=send_sem.at[block, flow],
+            recv_sem=recv_sem.at[block, flow, age],
             device_id={"dp": lax.rem(me + sign + n, n)},
             device_id_type=MESH,
         )
 
-    def arrived(p, way, age, kind):
-        copy = copy_of(p, way, age, kind)
-        copy.wait_send()
-        if kind == "sum":
-            copy.wait_recv()
-        else:
-            block, sign = WIDE * p + way, 1 - 2 * way
-            at = chunk(me - sign * (age - (n - 1) + 1))
-            pltpu.make_async_remote_copy(
-                src_ref=g_hbm.at[block, at],
-                dst_ref=g_hbm.at[block, at],
-                send_sem=send_sem.at[block],
-                recv_sem=recv_sem.at[block, age],
-                device_id={"dp": lax.rem(me + sign + n, n)},
-                device_id_type=MESH,
-            ).wait_recv()
-
-    def add(p, way, age):
-        block, sign = WIDE * p + way, 1 - 2 * way
-        at = chunk(me - sign * (age + 1))
-        total = (part[block, at].astype(F32) + recv[block, age - 1].astype(F32)).astype(BF16)
-        part[block, at] = total
-        return total
+    def sum_sent(block, sign, flow, hops, age):
+        source = part.at[block, chunk(me + sign * (hops - age))]
+        return copy_of(block, sign, flow, age, source, recv.at[block, flow * long + age])
+
+    def whole_sent(block, sign, flow, hop):
+        at, spare = part.at[block, chunk(me - sign * hop)], recv.at[block, flow * long]
+        source, target = spare if hop == 1 else at, spare if hop == 0 else at
+        return copy_of(block, sign, flow, long + hop, source, target)
+
+    def whole_received(block, sign, flow, hop):
+        at = recv.at[block, flow * long] if hop == 0 else part.at[block, chunk(me - sign * (hop + 1))]
+        return copy_of(block, sign, flow, long + hop, at, at)
 
     def keep(p, way):
         block = WIDE * p + way
-        return pltpu.make_async_copy(part.at[block, chunk(me)], g_hbm.at[block, chunk(me)], keep_sem.at[block])
-
-    def finish(p, way):
-        total = add(p, way, n - 1).astype(F32)
-        copy_of(p, way, n - 1, "first").start()
-        keep(p, way).start()
-        total = total * total
-        squares = own_squares[...]
-        for r in range(0, rows, 8):
-            for c in range(0, d, LANES):
-                squares = squares + total[r : r + 8, c : c + LANES]
-        own_squares[...] = squares
+        return pltpu.make_async_copy(part.at[block], g_hbm.at[block], keep_sem.at[block])
 
     def move(p, way, age):
-        last = 2 * (n - 1)
-
-        @pl.when(age == 0)
+        block = WIDE * p + way
+
+        for flow, hops in flows:
+            sign = (1 - 2 * way) * (1 - 2 * flow)
+
+            @pl.when((age >= 1) & (age <= hops))
+            def _():
+                copy = sum_sent(block, sign, flow, hops, age - 1)
+                copy.wait_send()
+                copy.wait_recv()
+
+            @pl.when((age >= 1) & (age < hops))
+            def _():
+                at = chunk(me + sign * (hops - age))
+                came = recv[block, flow * long + age - 1].astype(F32)
+                part[block, at] = (part[block, at].astype(F32) + came).astype(BF16)
+
+            @pl.when(age < hops)
+            def _():
+                sum_sent(block, sign, flow, hops, age).start()
+
+        @pl.when(age == long)
         def _():
-            copy_of(p, way, age, "sum").start()
-
-        @pl.when((age >= 1) & (age <= n - 1))
+            total = part[block, chunk(me)].astype(F32)
+            for flow, hops in flows:
+                total = total + recv[block, flow * long + hops - 1].astype(F32)
+            total = total.astype(BF16)
+            part[block, chunk(me)] = total
+            total = total.astype(F32)
+            total = total * total
+            squares = own_squares[...]
+            for r in range(0, rows, 8):
+                for c in range(0, d, LANES):
+                    squares = squares + total[r : r + 8, c : c + LANES]
+            own_squares[...] = squares
+
+        for flow, hops in flows:
+            sign = (1 - 2 * way) * (1 - 2 * flow)
+
+            for hop in range(hops + 1):
+
+                @pl.when(age == long + hop)
+                def _():
+                    if hop > 0:
+                        whole_sent(block, sign, flow, hop - 1).wait_send()
+                        whole_received(block, sign, flow, hop - 1).wait_recv()
+                    if hop == 1:
+                        part[block, chunk(me - sign)] = recv[block, flow * long]
+                    if hop < hops:
+                        whole_sent(block, sign, flow, hop).start()
+
+        @pl.when(age == last_age)
         def _():
-            arrived(p, way, age - 1, "sum")
-
-            @pl.when(age < n - 1)
+            keep(p, way).start()
+
+    first_steps = SLOTS[1] * per_layer
+    steps = first_steps + SLOTS[0] * per_layer
+
+    def sets_out(p):
+        return jnp.where(p < per_layer, SLOTS[1] * (p + 1), first_steps + SLOTS[0] * (p + 1 - per_layer))
+
+    in_flight = last_age // min(SLOTS) + 1
+
+    def slot(s, current):
+        def one(k, _):
+            p = current - in_flight + k
+            age = s - sets_out(p)
+
+            @pl.when((p >= 0) & (p < pieces) & (age <= last_age) & (age >= 0))
             def _():
-                add(p, way, age)
-                copy_of(p, way, age, "sum").start()
-
-            @pl.when(age == n - 1)
-            def _():
-                finish(p, way)
-
-        @pl.when(age == n)
-        def _():
-            arrived(p, way, age - 1, "first")
-
-        @pl.when((age > n) & (age <= last))
-        def _():
-            arrived(p, way, age - 1, "whole")
-
-        @pl.when((age >= n) & (age < last))
-        def _():
-            copy_of(p, way, age, "whole").start()
-
-        @pl.when(age == last)
-        def _():
-            keep(p, way).wait()
-
-    in_flight = -(-(2 * (n - 1) + 1) // SLOTS)
-
-    def slot(s):
-        def one(k, _):
-            q = in_flight - 1 - k
-            p, age = s // SLOTS - 1 - q, s % SLOTS + SLOTS * q
-
-            @pl.when((p >= 0) & (p < pieces))
-            def _():
-                @pl.when(p != pieces - 1)
-                def _():
-                    move(p, 0, age)
-
-                @pl.when(p != per_layer - 1)
+                move(p, 0, age)
+
+                @pl.when((p != per_layer - 1) & (p != pieces - 1))
                 def _():
                     move(p, 1, age)
 
@@ -234,8 +234,8 @@
         acc[...] = jnp.zeros_like(acc)
 
         def some(i, _):
-            for k in range(tiles // SLOTS):
-                at = pl.ds(pl.multiple_of((i * (tiles // SLOTS) + k) * tile, tile), tile)
+            for k in range(PAIR):
+                at = pl.ds(pl.multiple_of((i * PAIR + k) * tile, tile), tile)
                 w_gate, w_up, w_down = wg[layer, :, at_units], wu[layer, :, at_units], wd[layer, at_units, :]
                 a, back = a_ref[at], dh[at]
                 gate, up = nn(a, w_gate), nn(a, w_up)
@@ -254,15 +254,21 @@
                         dh[at] = (back.astype(F32) + normed_back(h1[at], total).astype(F32)).astype(BF16)
                     else:
                         da[at] = total
-            slot(p * SLOTS + i)
             return 0
 
-        lax.fori_loop(0, SLOTS, some, 0)
+        between = tiles // PAIR // SLOTS[layer]
+        before = sets_out(p) - SLOTS[layer]
+
+        def stretch(i, _):
+            lax.fori_loop(i * between, (i + 1) * between, some, 0)
+            slot(before + i, p)
+            return 0
+
+        lax.fori_loop(0, SLOTS[layer], stretch, 0)
         for half in range(wide):
-            way = half if wide == WIDE else 1 - layer
             for kind in range(KINDS):
                 first = kind * units + half * LANES
-                part[WIDE * p + way, kind * LANES : (kind + 1) * LANES] = acc[first : first + LANES].astype(BF16)
+                part[WIDE * p + half, kind * LANES : (kind + 1) * LANES] = acc[first : first + LANES].astype(BF16)
 
     def chunk_of(layer, j, _):
         base = (1 - layer) * per_layer
@@ -274,12 +280,10 @@
         compute(layer, (2 - layer) * per_layer - 1, (blocks - 1) * LANES, 1, True)
 
     def rest(s, _):
-        slot(s)
+        slot(s, pieces)
         return 0
 
-    done = SLOTS * (pieces + 1) + 2 * (n - 1) + 1
-    summed = SLOTS * (pieces + 1) - SLOTS + n + SLOTS
-    lax.fori_loop(SLOTS * pieces, summed, rest, 0)
+    lax.fori_loop(steps, steps + long + 1, rest, 0)
 
     def squares_to(away):
         return pltpu.make_async_remote_copy(
@@ -304,7 +308,7 @@
     for away in range(1, n):
         squares_to(away).start()
     all_squares[me] = own_squares[...]
-    lax.fori_loop(summed, done, rest, 0)
+    lax.fori_loop(steps + long + 1, steps + last_age + 1, rest, 0)
     for away in range(1, n):
         squares_to(away).wait_send()
         squares_from(away).wait_recv()
@@ -312,6 +316,15 @@
     for i in range(1, n):
         total = total + all_squares[i]
     squares_ref[...] = total
+
+    def kept(block, _):
+        @pl.when((block != WIDE * per_layer - 1) & (block != WIDE * pieces - 1))
+        def _():
+            keep(0, block).wait()
+
+        return 0
+
+    lax.fori_loop(0, WIDE * pieces, kept, 0)
 
 
 def gradients(n, tiles, x, dy, w_gate, w_up, w_down):
@@ -339,7 +352,7 @@
             pltpu.VMEM((8, LANES), F32),
             pltpu.VMEM((n, 8, LANES), F32),
             dma((tiles,)), dma((tiles,)), dma((layers, KINDS)),
-            dma((blocks,)), dma((blocks, 2 * (n - 1))), dma((blocks,)),
+            dma((blocks, 2)), dma((blocks, 2, 2 * (n // 2))), dma((blocks,)),
             dma((n,)), dma((n,)),
         ],
         compiler_params=pltpu.CompilerParams(
@@ -349,47 +362,47 @@
     )(x, dy, w_gate, w_up, w_down)
 
 
-def step_kernel(count, squares_ref, g1_ref, g0_ref, *refs):
+def step_kernel(count, squares_ref, g_ref, *refs):
     old, new = refs[:9], refs[9:]
     mean = jnp.sum(jnp.sum(squares_ref[...], 0, keepdims=True), 1, keepdims=True) / count
     factor = jnp.minimum(1.0, 0.5 * lax.rsqrt(mean + 1e-30))
     for i, kind in enumerate((1, 2, 0)):
-        for layer, g_ref in ((0, g0_ref), (1, g1_ref)):
-            g = g_ref[0, kind * LANES : (kind + 1) * LANES, :].astype(F32)
-            if kind:
-                g = g.T
-            g = g * factor
-            m = 0.9 * old[3 + i][layer] + 0.1 * g
-            v = 0.95 * old[6 + i][layer] + 0.05 * g * g
-            w = old[i][layer].astype(F32)
-            new[i][layer] = (w - 0.02 * (m * lax.rsqrt(v + 1e-8) + 0.1 * w)).astype(BF16)
-            new[3 + i][layer] = m
-            new[6 + i][layer] = v
+        for half in range(WIDE):
+            g = g_ref[half, kind * LANES : (kind + 1) * LANES, :].astype(F32)
+            units = slice(half * LANES, (half + 1) * LANES)
+            at = (0, slice(None), units) if kind else (0, units)
+            g = (g.T if kind else g) * factor
+            m = 0.9 * old[3 + i][at] + 0.1 * g
+            v = 0.95 * old[6 + i][at] + 0.05 * g * g
+            w = old[i][at].astype(F32)
+            new[i][at] = (w - 0.02 * (m * lax.rsqrt(v + 1e-8) + 0.1 * w)).astype(BF16)
+            new[3 + i][at] = m
+            new[6 + i][at] = v
 
 
 def take_step(summed, squares, weights, m, v):
     layers, d, ff = weights[0].shape
-    blocks = ff // LANES
+    units = WIDE * LANES
+    pieces = pl.cdiv(ff, units)
     count = float(sum(w.size for w in weights))
-    by_columns = pl.BlockSpec((layers, d, LANES), lambda f: (0, 0, f))
-    by_rows = pl.BlockSpec((layers, LANES, d), lambda f: (0, f, 0))
+    by_columns = pl.BlockSpec((1, d, units), lambda layer, j: (layer, 0, j))
+    by_rows = pl.BlockSpec((1, units, d), lambda layer, j: (layer, j, 0))
     arrays = [by_columns, by_columns, by_rows] * 3
-    block = (1, KINDS * LANES, d)
-    half = summed.shape[0] // 2
     return pl.pallas_call(
         functools.partial(step_kernel, count),
-        grid=(blocks,),
+        grid=(layers, pieces),
         out_shape=[jax.ShapeDtypeStruct(a.shape, a.dtype) for a in (*weights, *m, *v)],
         in_specs=[
-            pl.BlockSpec((8, LANES), lambda f: (0, 0)),
-            pl.BlockSpec(block, lambda f: (f, 0, 0)),
-            pl.BlockSpec(block, lambda f: (half + f + f // (blocks - 1), 0, 0)),
+            pl.BlockSpec((8, LANES), lambda layer, j: (0, 0)),
+            pl.BlockSpec((WIDE, KINDS * LANES, d), lambda layer, j: ((layers - 1 - layer) * pieces + j, 0, 0)),
             *arrays,
         ],
         out_specs=arrays,
-        compiler_params=pltpu.CompilerParams(dimension_semantics=("arbitrary",), vmem_limit_bytes=50_000_000),
+        compiler_params=pltpu.CompilerParams(
+            dimension_semantics=("arbitrary", "arbitrary"), vmem_limit_bytes=67_043_328
+        ),
         name="step",
-    )(squares, summed, summed, *weights, *m, *v)
+    )(squares, summed, *weights, *m, *v)
 
 
 def solution(mesh, tiles=8):

time: 373 us -> 324 us (0.87)
  Pallas kernels: 370 us -> 323 us
    pallas_call x1, Pallas kernels: 328 us -> 281 us  [gradients(): pl.pallas_call(functools.partial(gradients_kernel, n), out_shape=(jax.Sha...]
where the time goes in v2:
time: 324 us
  Pallas kernels  323 us (100%)
    pallas_call x1, Pallas kernels, gradients(): pl.pallas_call(functools.partial(gradients_kernel, n), out_shape=(jax.Sha...  281 us
    pallas_call x1, Pallas kernels, take_step(): pl.pallas_call(functools.partial(step_kernel, count), grid=(layers, piece...  42.1 us

profile of v2, /device:TPU:30, one launch (start us, length us, event | category | flops | bytes accessed | tf_op | source)
XLA Modules:
  0.0 323.9 jit_solution(11690971753570516368)
XLA Ops:
  0.6 281.0 %gradients.1 = (bf16[28,384,512]{2,1,0:T(8,128)(2,1)}, f32[8,128]{1,0:T(8,128)}) custom-call(bf16[4096,512]{1,0:T(8,128)(2,1)} %bitcast.2, bf16[4096,512]{1,0:T(8,128)(2,1)} %bitcast.3, bf16[2,512,1664]{2,1,0:T(8,128)(2,1)} %refs_0_.1, bf16[2,512,1664]{2,1,0:T(8,128)(2,1)} %refs_1_.1, bf16[2,1664,512]{2,1,0:T(8,128)(2,1)} %refs_2_.1), custom_call_target="tpu_custom_call" | custom-call | tf_op jit(solution)/shard_map/gradients/pallas_call | solution.py:337
  281.6 42.1 %step.1 = (bf16[2,512,1664]{2,1,0:T(8,128)(2,1)}, bf16[2,512,1664]{2,1,0:T(8,128)(2,1)}, bf16[2,1664,512]{2,1,0:T(8,128)(2,1)}, f32[2,512,1664]{2,1,0:T(8,128)},...) custom-call(f32[8,128]{1,0:T(8,128)} %get-tuple-element.11.squares_r, ...), custom_call_target="tpu_custom_call" | custom-call | tf_op jit(solution)/shard_map/step/pallas_call | solution.py:391

commit v3 on v2

--- a/solution.py
+++ b/solution.py
@@ -202,11 +202,11 @@
         def _():
             keep(p, way).start()
 
-    first_steps = SLOTS[1] * per_layer
+    first_steps = SLOTS[1] * (per_layer + 1)
     steps = first_steps + SLOTS[0] * per_layer
 
     def sets_out(p):
-        return jnp.where(p < per_layer, SLOTS[1] * (p + 1), first_steps + SLOTS[0] * (p + 1 - per_layer))
+        return jnp.where(p < per_layer, SLOTS[1] * (p + 1 + jnp.minimum(p, 1)), first_steps + SLOTS[0] * (p + 1 - per_layer))
 
     in_flight = last_age // min(SLOTS) + 1
 
@@ -256,15 +256,16 @@
                         da[at] = total
             return 0
 
-        between = tiles // PAIR // SLOTS[layer]
-        before = sets_out(p) - SLOTS[layer]
+        count = SLOTS[layer] * (1 + (p == 1)) if layer == 1 else SLOTS[layer]
+        between = tiles // PAIR // count
+        before = sets_out(p) - count
 
         def stretch(i, _):
+            slot(before + i, p)
             lax.fori_loop(i * between, (i + 1) * between, some, 0)
-            slot(before + i, p)
             return 0
 
-        lax.fori_loop(0, SLOTS[layer], stretch, 0)
+        lax.fori_loop(0, count, stretch, 0)
         for half in range(wide):
             for kind in range(KINDS):
                 first = kind * units + half * LANES

time: 324 us -> 316 us (0.975)
  Pallas kernels: 323 us -> 315 us
    pallas_call x1, Pallas kernels: 281 us -> 273 us  [gradients(): pl.pallas_call(functools.partial(gradients_kernel, n), out_shape=(jax.Sha...]
where the time goes in v3:
time: 316 us
  Pallas kernels  315 us (100%)
    pallas_call x1, Pallas kernels, gradients(): pl.pallas_call(functools.partial(gradients_kernel, n), out_shape=(jax.Sha...  273 us
    pallas_call x1, Pallas kernels, take_step(): pl.pallas_call(functools.partial(step_kernel, count), grid=(layers, piece...  42.1 us

profile of v3, /device:TPU:30, one launch (start us, length us, event | category | flops | bytes accessed | tf_op | source)
XLA Modules:
  0.0 316.0 jit_solution(5023566511397783367)
XLA Ops:
  0.6 273.0 %gradients.1 = (bf16[28,384,512]{2,1,0:T(8,128)(2,1)}, f32[8,128]{1,0:T(8,128)}) custom-call(bf16[4096,512]{1,0:T(8,128)(2,1)} %bitcast.2, bf16[4096,512]{1,0:T(8,128)(2,1)} %bitcast.3, bf16[2,512,1664]{2,1,0:T(8,128)(2,1)} %refs_0_.1, bf16[2,512,1664]{2,1,0:T(8,128)(2,1)} %refs_1_.1, bf16[2,1664,512]{2,1,0:T(8,128)(2,1)} %refs_2_.1), custom_call_target="tpu_custom_call" | custom-call | tf_op jit(solution)/shard_map/gradients/pallas_call | solution.py:338
  273.7 42.1 %step.1 = (bf16[2,512,1664]{2,1,0:T(8,128)(2,1)}, bf16[2,512,1664]{2,1,0:T(8,128)(2,1)}, bf16[2,1664,512]{2,1,0:T(8,128)(2,1)}, f32[2,512,1664]{2,1,0:T(8,128)},...) custom-call(f32[8,128]{1,0:T(8,128)} %get-tuple-element.11.squares_r, ...), custom_call_target="tpu_custom_call" | custom-call | tf_op jit(solution)/shard_map/step/pallas_call | solution.py:392
